TPU v7x, 1024 devices: a whole 4x4x32 slice. The times are simulated.
1024 devices in a mesh: sp: 32 (over y, x, core), dp: 32 (over z).
Axes of the slice: x: 4, y: 4, z: 32, core: 2. Of those that a mesh axis runs over, the one named last changes fastest.
Arguments:
- hidden: bfloat16 [32, 8192, 4096], P('dp', 'sp'), may hold values from -24 to 24
- pad_counts: int32 [32, 32], P('dp', 'sp'), may hold values from 64 to 128
- doc_lengths: int32 [32, 128], P('dp'), may hold values from 1 to 128, 8192 in all within a row
- range_shift: int32 [32, 32], P('dp'), may hold values from -32 to 32
- qkv_weight: bfloat16 [4096, 384], P('dp'), may hold values from -0.09375 to 0.09375
Outputs:
- attended: bfloat16 [32, 8192, 128], P('dp', 'sp')
Inputs may be any that keep to these rules, and one draw needn't show every extreme that they name: `doc_lengths`: each row sums to 8192.
All inputs are finite; a program needn't handle non-finite values.
Results may differ from a plain program's by a relative error of at most 0.0095.
Values may be sent and summed in bfloat16 or wider, within the bound.
No kernel may reach another device: no remote copies, remote signals or barrier semaphores. Data moves between devices by JAX's collectives and lax.ppermute only.
A program may use at most 32 MiB of HBM per device.

v0:
```python
import math

import jax
import jax.numpy as jnp
from jax import lax
from jax.experimental import pallas as pl
from jax.experimental.pallas import tpu as pltpu
from jax.sharding import Mesh
from jax.sharding import PartitionSpec as P

PLANE = ("y", "x", "core")
EDGE = 32
SIDE = 4
STEPS = (0, 1, 3, 2)
NEAR = [d for k in range(8) for _ in range(2) for d in ((k, -k) if k else (0, 8))]
FAR = [d for k in range(8) for _ in range(2) for d in ((16 - k, k - 16) if k else (16, -8))]
SHIFTS = (NEAR, FAR)
SMALL = pltpu.CompilerParams(vmem_limit_bytes=16 * 1024 * 1024)


def distance(k, side, kind):
    if kind == 0:
        return jnp.where(side == 0, k, jnp.where(k == 0, 8, -k))
    return jnp.where(side == 0, 16 - k, jnp.where(k == 0, -8, k - 16))


def project_half(side, at, plane, sources, blocks):
    lanes = blocks[0].shape[2]
    planes = sources[0].shape[1] // lanes
    deep = (blocks[0].shape[1] - 8) // 6
    total = None
    for step, block in zip(STEPS, blocks):
        line = lax.rem(at + SIDE - step, SIDE)
        for pair in range(SIDE // 2):
            inputs, weights = [], []
            for kind in range(2):
                shift = distance(SIDE // 2 * line + pair, side, kind)
                shard = lax.rem(plane + planes - shift, planes)
                columns = pl.ds(pl.multiple_of(shard * lanes, lanes), lanes)
                inputs.append(jnp.concatenate([rows[:, columns] for rows in sources], axis=0))
                first = kind * 3 * deep
                for place in (2 * pair, 2 * pair + 1):
                    weights.append(
                        jnp.concatenate(
                            [
                                block[place, first + i * deep : first + (i + 1) * deep]
                                for i in range(3)
                            ],
                            axis=1,
                        )
                    )
            part = jnp.dot(
                jnp.concatenate(inputs, axis=1),
                jnp.concatenate(weights, axis=0),
                preferred_element_type=jnp.float32,
            )
            total = part if total is None else total + part
    return total


def tokens_before(side, at, index, blocks):
    last = blocks[0].shape[1] - 8
    total = jnp.zeros((8, blocks[0].shape[2]), jnp.float32)
    for step, block in zip(STEPS, blocks):
        line = lax.rem(at + SIDE - step, SIDE)
        for place in range(SIDE):
            chip = jnp.where(side == 0, SIDE * line + place, SIDE * place + line)
            owner = 2 * chip + lax.rem(side + line + place, 2)
            total += jnp.where(owner < index, block[place, last:].astype(jnp.float32), 0.0)
    return total


def parts_of(joined, last):
    return [joined.at[i * SIDE : (i + 1) * SIDE] for i in range(SIDE - 1)] + [last]


def project_kernel(
    scalars, slots, left, right, lengths, joined, last, projected, before, ends
):
    side, at, _, plane, index = (scalars[i] for i in range(5))
    blocks = parts_of(joined, last)
    projected[...] = project_half(side, at, plane, (slots, left, right), blocks)
    before[...] = tokens_before(side, at, index, blocks)
    total = jnp.broadcast_to(lengths[...], ends.shape)
    lane = lax.broadcasted_iota(jnp.int32, ends.shape, 1)
    reach = 1
    while reach < ends.shape[1]:
        total += jnp.where(lane >= reach, pltpu.roll(total, reach, 1), 0)
        reach *= 2
    ends[...] = total


def project(scalars, slots, left, right, lengths, joined, last):
    rows = slots.shape[0] + left.shape[0] + right.shape[0]
    lanes = last.shape[2]
    return pl.pallas_call(
        project_kernel,
        out_shape=(
            jax.ShapeDtypeStruct((rows, 3 * lanes), jnp.float32),
            jax.ShapeDtypeStruct((8, lanes), jnp.float32),
            jax.ShapeDtypeStruct((8, lengths.shape[1]), jnp.int32),
        ),
        in_specs=[pl.BlockSpec(memory_space=pltpu.SMEM)]
        + [pl.BlockSpec(memory_space=pltpu.VMEM)] * 6,
        out_specs=(pl.BlockSpec(memory_space=pltpu.VMEM),) * 3,
        compiler_params=SMALL,
        cost_estimate=pl.CostEstimate(
            flops=3 * rows * slots.shape[1] * lanes, bytes_accessed=0, transcendentals=0
        ),
        name="project",
    )(scalars, slots, left, right, lengths, joined, last)


def attend_kernel(
    scalars, pads, shifts, slots, left, right, projected, before, ends, joined, last, attended
):
    blocks = parts_of(joined, last)
    rows, head_dim = attended.shape
    side, _, at, plane, index = (scalars[i] for i in range(5))
    devices = shifts.shape[1]
    padding = pads[0, 0]
    held = rows - padding
    shift = jnp.where(index == 0, 0, shifts[0, index])
    following = shifts[0, jnp.minimum(index + 1, devices - 1)]
    count = held - shift + jnp.where(index == devices - 1, 0, following)
    before = before[...] + tokens_before(1 - side, at, index, blocks)
    start = before[:1, :1].astype(jnp.int32) + shift
    sources = (slots, left, right)
    projected = (projected[...] + project_half(1 - side, at, plane, sources, blocks)).astype(
        jnp.bfloat16
    )
    row = lax.broadcasted_iota(jnp.int32, (rows, 1), 0)
    live = row < count
    offset = row + shift
    source = jnp.where(
        offset < 0,
        rows + EDGE + offset,
        jnp.where(offset < held, padding + offset, rows + EDGE + offset - held),
    )
    source = jnp.where(live, source, -1)
    columns = lax.broadcasted_iota(jnp.int32, (rows, projected.shape[0]), 1)
    picked = jnp.where(columns == source, 1.0, 0.0).astype(jnp.bfloat16)
    projected = jnp.dot(picked, projected, preferred_element_type=jnp.float32).astype(
        jnp.bfloat16
    )
    query, keys, values = (projected[:, i * head_dim : (i + 1) * head_dim] for i in range(3))
    scores = lax.dot_general(
        query, keys, (((1,), (1,)), ((), ())), preferred_element_type=jnp.float32
    ) / math.sqrt(head_dim)
    key = lax.broadcasted_iota(jnp.int32, (rows, rows), 1)
    passed = jnp.where(ends[:1] <= row + start, ends[:1], 0)
    opened = jnp.max(passed, axis=1, keepdims=True) - start
    allowed = (key <= row) & (key >= opened) & live
    masked = jnp.where(allowed, scores, -1e30)
    peak = jnp.max(masked, axis=1, keepdims=True)
    exponent = jnp.where(allowed, jnp.exp(masked - peak), 0.0)
    denominator = jnp.sum(exponent, axis=1, keepdims=True)
    probs = (exponent / jnp.where(live, denominator, 1.0)).astype(jnp.bfloat16)
    result = jnp.dot(probs, values, preferred_element_type=jnp.float32)
    attended[...] = jnp.where(live, result, 0.0).astype(jnp.bfloat16)


def attend(scalars, pads, shifts, slots, left, right, projected, before, ends, joined, last):
    return pl.pallas_call(
        attend_kernel,
        out_shape=jax.ShapeDtypeStruct((slots.shape[0], last.shape[2]), jnp.bfloat16),
        in_specs=[pl.BlockSpec(memory_space=pltpu.SMEM)] * 3
        + [pl.BlockSpec(memory_space=pltpu.VMEM)] * 8,
        out_specs=pl.BlockSpec(memory_space=pltpu.VMEM),
        compiler_params=SMALL,
        name="attend",
    )(scalars, pads, shifts, slots, left, right, projected, before, ends, joined, last)


def join_kernel(*refs):
    places = refs[0].shape[0]
    for at, block in enumerate(refs[:-1]):
        refs[-1][at * places : (at + 1) * places] = block[...]


def join(blocks):
    places, deep, lanes = blocks[0].shape
    return pl.pallas_call(
        join_kernel,
        out_shape=jax.ShapeDtypeStruct((len(blocks) * places, deep, lanes), jnp.bfloat16),
        in_specs=[pl.BlockSpec(memory_space=pltpu.VMEM)] * len(blocks),
        out_specs=pl.BlockSpec(memory_space=pltpu.VMEM),
        compiler_params=SMALL,
        name="join",
    )(*blocks)


def for_each(value, count):
    return jnp.broadcast_to(value[None], (count, *value.shape))


def device(place, side):
    chip = place if side == 0 else place % SIDE * SIDE + place // SIDE
    return 2 * chip + (side + chip % SIDE + chip // SIDE) % 2


def moved(value, kind):
    planes = lax.axis_size("z")
    pairs = [
        (device(place, side) * planes + z, device(place, side) * planes + (z + shift) % planes)
        for place in range(SIDE * SIDE)
        for side, shift in enumerate(SHIFTS[kind][2 * place : 2 * place + 2])
        for z in range(planes)
    ]
    return lax.ppermute(value, (*PLANE, "z"), pairs)


def line_of(value):
    groups = [
        [device(SIDE * at + place, side) for place in range(SIDE)]
        for at in range(SIDE)
        for side in range(2)
    ]
    return lax.all_to_all(
        for_each(value, SIDE), PLANE, 0, 0, axis_index_groups=groups, tiled=True
    )


def passed_on(value, step):
    pairs = [
        (device(place, side), device((place + SIDE * step) % SIDE**2, side))
        for place in range(SIDE**2)
        for side in range(2)
    ]
    return lax.ppermute(value, PLANE, pairs)


def shards(hidden, pad_counts, doc_lengths, range_shift, qkv_weight):
    slots = hidden[0]
    rows = slots.shape[0]
    size, index = lax.axis_size(PLANE), lax.axis_index(PLANE)
    padding = pad_counts[0, 0]
    live = rows - padding

    deep = qkv_weight.shape[0] // 2
    x, y = lax.axis_index("x"), lax.axis_index("y")
    side = (lax.axis_index("core") + x + y) % 2
    upper = jnp.where(side == 0, x, y) % 2
    own = lax.dynamic_slice_in_dim(qkv_weight, upper * deep, deep, 0)
    own = jnp.concatenate(jnp.split(own, 3, axis=1), axis=0)
    far = moved(own, 1)
    head = lax.dynamic_slice_in_dim(slots, padding, EDGE, 0)
    tail = slots[rows - EDGE :]
    left = lax.ppermute(tail, PLANE, [(i, i + 1) for i in range(size - 1)])
    right = lax.ppermute(head, PLANE, [(i + 1, i) for i in range(size - 1)])
    near = moved(own, 0)

    scalars = jnp.stack(
        [
            side,
            jnp.where(side == 0, y, x),
            jnp.where(side == 0, x, y),
            lax.axis_index("z"),
            index,
        ]
    ).astype(jnp.int32)
    near, far, scalars = lax.optimization_barrier((near, far, scalars))
    tally = jnp.full((8, own.shape[1]), live).astype(jnp.bfloat16)
    line = line_of(jnp.concatenate([near, far, tally]))
    after = passed_on(line, 1)
    ahead = passed_on(line, 3)
    lower = passed_on(after[: SIDE // 2], 1)
    higher = passed_on(ahead[SIDE // 2 :], 3)
    joined, last = join([line, after, ahead]), join([lower, higher])
    mates = [(0, 1), (1, 0)]
    other_joined = lax.ppermute(joined, "core", mates)
    other_last = lax.ppermute(last, "core", mates)
    projected, before, ends = project(
        scalars, slots, left, right, doc_lengths, joined, last
    )
    return attend(
        scalars,
        pad_counts,
        range_shift,
        slots,
        left,
        right,
        projected,
        before,
        ends,
        other_joined,
        other_last,
    )[None]


def solution(mesh):
    fine = Mesh(mesh.devices.reshape(4, 4, 2, -1), ("y", "x", "core", "z"))
    in_specs = (P("z", PLANE, None), P("z", PLANE), P("z", None), P("z", None), P("z", None))
    return jax.shard_map(
        shards, mesh=fine, in_specs=in_specs, out_specs=P("z", PLANE, None), check_vma=False
    )
```

profile of v0, /device:TPU:8, one launch (start us, length us, event | category | flops | bytes accessed | tf_op | source)
XLA Modules:
  0.0 94.3 jit_solution(11034756879866174831)
XLA Ops:
  0.0 0.8 constant_dynamic-slice_fusion
  0.8 23.0 %collective-permute-start.1 = (bf16[192,128]{1,0:T(8,128)(2,1)S(1)}, bf16[192,128]{1,0:T(8,128)(2,1)S(1)}, u32[]{:S(2)}, u32[]{:S(2)}) collective-permute-start(bf16[192,128]{1,0:T(8,128)(2,1)S(1)} %pad_maximum_fusion), channel_id=1, source_target_pairs={{0,16},{1,17},{2,18},{3,19},{4,20},{5,21},{6,22},{7,23},{8,24},{9,... | collective-permute-start | bytes 147464 | tf_op jit(solution)/shard_map/ppermute | solution.py:210
  23.8 1.9 %collective-permute-start = (bf16[192,128]{1,0:T(8,128)(2,1)S(1)}, bf16[192,128]{1,0:T(8,128)(2,1)S(1)}, u32[]{:S(2)}, u32[]{:S(2)}) collective-permute-start(bf16[192,128]{1,0:T(8,128)(2,1)S(1)} %pad_maximum_fusion), channel_id=1, source_target_pairs={{0,0},{1,1},{2,2},{3,3},{4,4},{5,5},{6,6},{7,7},{8,8},{9,9},{10,10... | collective-permute-start | bytes 147464 | tf_op jit(solution)/shard_map/ppermute | solution.py:210
  26.4 0.1 stack.23.scalars
  26.5 12.2 %collective-permute-done = bf16[192,128]{1,0:T(8,128)(2,1)S(1)} collective-permute-done((bf16[192,128]{1,0:T(8,128)(2,1)S(1)}, bf16[192,128]{1,0:T(8,128)(2,1)S(1)}, u32[]{:S(2)}, u32[]{:S(2)}) %collective-permute-start) | collective-permute-done | bytes 49184 | tf_op jit(solution)/shard_map/ppermute | solution.py:210
  38.7 0.1 maximum_maximum_fusion
  38.8 0.1 broadcast_in_dim.13
  38.9 11.3 %all_to_all.5.refs_0_ = bf16[4,392,128]{2,1,0:T(8,128)(2,1)S(1)} all-to-all(bf16[4,392,128]{2,1,0:T(8,128)(2,1)S(1)} %broadcast_in_dim.13), channel_id=1, replica_groups={{0,96,128,224},{32,256,544,768},{288,320,416,448},{64,352,576,864},{512..., dimensions={0} | all-to-all | bytes 802816 | tf_op jit(solution)/shard_map/all_to_all | solution.py:219
  50.2 2.8 %collective-permute-start.5 = (bf16[4,392,128]{2,1,0:T(8,128)(2,1)S(1)}, bf16[4,392,128]{2,1,0:T(8,128)(2,1)S(1)}, u32[]{:S(2)}, u32[]{:S(2)}) collective-permute-start(bf16[4,392,128]{2,1,0:T(8,128)(2,1)S(1)} %all_to_all.5.refs_0_), channel_id=1, source_target_pairs={{0,800},{32,192},{96,832},{256,480},{128,928},{544,704},{224,960},... | collective-permute-start | bytes 1204232 | tf_op jit(solution)/shard_map/ppermute | solution.py:230
  53.0 3.3 %collective-permute-start.4 = (bf16[4,392,128]{2,1,0:T(8,128)(2,1)S(1)}, bf16[4,392,128]{2,1,0:T(8,128)(2,1)S(1)}, u32[]{:S(2)}, u32[]{:S(2)}) collective-permute-start(bf16[4,392,128]{2,1,0:T(8,128)(2,1)S(1)} %all_to_all.5.refs_0_), channel_id=1, source_target_pairs={{0,288},{32,64},{96,320},{256,352},{128,416},{544,576},{224,448},{... | collective-permute-start | bytes 1204232 | tf_op jit(solution)/shard_map/ppermute | solution.py:230
  56.3 3.6 %collective-permute-done.5.refs_2_ = bf16[4,392,128]{2,1,0:T(8,128)(2,1)S(1)} collective-permute-done((bf16[4,392,128]{2,1,0:T(8,128)(2,1)S(1)}, bf16[4,392,128]{2,1,0:T(8,128)(2,1)S(1)}, u32[]{:S(2)}, u32[]{:S(2)}) %collective-permute-start.5) | collective-permute-done | bytes 401440 | tf_op jit(solution)/shard_map/ppermute | solution.py:230
  59.9 0.7 slice.17
  60.6 3.5 %collective-permute-start.7 = (bf16[2,392,128]{2,1,0:T(8,128)(2,1)}, bf16[2,392,128]{2,1,0:T(8,128)(2,1)S(1)}, u32[]{:S(2)}, u32[]{:S(2)}) collective-permute-start(bf16[2,392,128]{2,1,0:T(8,128)(2,1)} %slice.17), channel_id=1, source_target_pairs={{0,800},{32,192},{96,832},{256,480},{128,928},{544,704},{224,960},... | collective-permute-start | bytes 602120 | tf_op jit(solution)/shard_map/ppermute | solution.py:230
  64.0 0.0 collective-permute-done.4.refs_1_
  64.1 0.7 slice.16
  64.8 2.1 %collective-permute-start.6 = (bf16[2,392,128]{2,1,0:T(8,128)(2,1)}, bf16[2,392,128]{2,1,0:T(8,128)(2,1)}, u32[]{:S(2)}, u32[]{:S(2)}) collective-permute-start(bf16[2,392,128]{2,1,0:T(8,128)(2,1)} %slice.16), channel_id=1, source_target_pairs={{0,288},{32,64},{96,320},{256,352},{128,416},{544,576},{224,448},{... | collective-permute-start | bytes 602120 | tf_op jit(solution)/shard_map/ppermute | solution.py:230
  66.8 0.0 copy-start.1
  66.9 0.1 join.2.joined
  66.9 1.9 %collective-permute-start.8 = (bf16[12,392,128]{2,1,0:T(8,128)(2,1)S(1)}, bf16[12,392,128]{2,1,0:T(8,128)(2,1)S(1)}, u32[]{:S(2)}, u32[]{:S(2)}) collective-permute-start(bf16[12,392,128]{2,1,0:T(8,128)(2,1)S(1)} %join.2.joined), channel_id=1, source_target_pairs={{0,32},{32,0},{1,33},{33,1},{2,34},{34,2},{3,35},{35,3},{4,36},{36... | collective-permute-start | bytes 3612680 | tf_op jit(solution)/shard_map/ppermute | solution.py:271
  68.9 0.0 collective-permute-done.7.refs_1_
  68.9 4.4 %collective-permute-done.6.refs_0_ = bf16[2,392,128]{2,1,0:T(8,128)(2,1)} collective-permute-done((bf16[2,392,128]{2,1,0:T(8,128)(2,1)}, bf16[2,392,128]{2,1,0:T(8,128)(2,1)}, u32[]{:S(2)}, u32[]{:S(2)}) %collective-permute-start.6) | collective-permute-done | bytes 200736 | tf_op jit(solution)/shard_map/ppermute | solution.py:230
  73.3 1.0 %join.3.last = bf16[4,392,128]{2,1,0:T(8,128)(2,1)S(1)} custom-call(bf16[2,392,128]{2,1,0:T(8,128)(2,1)} %collective-permute-done.6.refs_0_, bf16[2,392,128]{2,1,0:T(8,128)(2,1)S(1)} %collective-permute-done.7.refs_1_), custom_call_target="tpu_custom_call" | custom-call | tf_op jit(solution)/shard_map/join/pallas_call | solution.py:183
  74.3 1.9 %collective-permute-start.9 = (bf16[4,392,128]{2,1,0:T(8,128)(2,1)S(1)}, bf16[4,392,128]{2,1,0:T(8,128)(2,1)S(1)}, u32[]{:S(2)}, u32[]{:S(2)}) collective-permute-start(bf16[4,392,128]{2,1,0:T(8,128)(2,1)S(1)} %join.3.last), channel_id=1, source_target_pairs={{0,32},{32,0},{1,33},{33,1},{2,34},{34,2},{3,35},{35,3},{4,36},{36... | collective-permute-start | bytes 1204232 | tf_op jit(solution)/shard_map/ppermute | solution.py:272
  76.2 0.1 dynamic-slice_bitcast_fusion
  76.3 3.9 %collective-permute-start.3 = (bf16[32,4096]{1,0:T(8,128)(2,1)S(1)}, bf16[32,4096]{1,0:T(8,128)(2,1)S(1)}, u32[]{:S(2)}, u32[]{:S(2)}) collective-permute-start(bf16[32,4096]{1,0:T(8,128)(2,1)S(1)} %get-tuple-element.17), channel_id=1, source_target_pairs={{32,0},{64,32},{96,64},{128,96},{160,128},{192,160},{224,192},{256... | collective-permute-start | bytes 786440 | tf_op jit(solution)/shard_map/ppermute | solution.py:250
  80.2 1.9 %collective-permute-start.2 = (bf16[32,4096]{1,0:T(8,128)(2,1)S(1)}, bf16[32,4096]{1,0:T(8,128)(2,1)S(1)}, u32[]{:S(2)}, u32[]{:S(2)}) collective-permute-start(bf16[32,4096]{1,0:T(8,128)(2,1)S(1)} %get-tuple-element.18), channel_id=1, source_target_pairs={{0,32},{32,64},{64,96},{96,128},{128,160},{160,192},{192,224},{224... | collective-permute-start | bytes 786440 | tf_op jit(solution)/shard_map/ppermute | solution.py:249
  82.1 1.9 %collective-permute-done.3.right = bf16[32,4096]{1,0:T(8,128)(2,1)S(1)} collective-permute-done((bf16[32,4096]{1,0:T(8,128)(2,1)S(1)}, bf16[32,4096]{1,0:T(8,128)(2,1)S(1)}, u32[]{:S(2)}, u32[]{:S(2)}) %collective-permute-start.3) | collective-permute-done | bytes 262176 | tf_op jit(solution)/shard_map/ppermute | solution.py:250
  84.1 5.9 %collective-permute-done.2.left = bf16[32,4096]{1,0:T(8,128)(2,1)S(1)} collective-permute-done((bf16[32,4096]{1,0:T(8,128)(2,1)S(1)}, bf16[32,4096]{1,0:T(8,128)(2,1)S(1)}, u32[]{:S(2)}, u32[]{:S(2)}) %collective-permute-start.2) | collective-permute-done | bytes 262176 | tf_op jit(solution)/shard_map/ppermute | solution.py:249
  90.0 1.4 %project.1 = (f32[320,384]{1,0:T(8,128)S(1)}, f32[8,128]{1,0:T(8,128)S(1)}, s32[8,128]{1,0:T(8,128)S(1)}) custom-call(s32[5]{0:T(128)S(1)} %stack.23.scalars, bf16[256,4096]{1,0:T(8,128)(2,1)S(1)} %bitcast.16, bf16[32,4096]{1,0:T(8,128)(2,1)S(1)} %collective-permute-done.2.left, bf16[32,4096]{1,0:T(8,128)(2,1)S(1)} %collective-permute-done.3.right, ...), custom_call_target="tpu_custom_call" | custom-call | flops 503316480 | tf_op jit(solution)/shard_map/project/pallas_call | solution.py:96
  91.4 0.0 collective-permute-done.9.last
  91.4 0.0 collective-permute-done.8.joined
  91.4 2.8 %attend.1 = bf16[256,128]{1,0:T(8,128)(2,1)} custom-call(s32[5]{0:T(128)S(1)} %stack.23.scalars, s32[1,1]{1,0:T(1,128)} %copy.6.pads, s32[1,32]{1,0:T(1,128)S(1)} %copy-done.2, bf16[256,4096]{1,0:T(8,128)(2,1)S(1)} %bitcast.17, bf16[32,4096]{1,0:T(8,128)(2,1)S(1)} %collective-permute-done.2.left, bf16[32,4096]{1,0:T(8,128)(2,1)S(1)} %collective-permute-done.3.right, ...), custom_call_target="tpu_custom_call" | custom-call | tf_op jit(solution)/shard_map/attend/pallas_call | solution.py:164
  (9 shorter events, 0.0 us)
Async XLA Ops:
  0.8 25.7 %collective-permute-start.1 = (bf16[192,128]{1,0:T(8,128)(2,1)S(1)}, bf16[192,128]{1,0:T(8,128)(2,1)S(1)}, u32[]{:S(2)}, u32[]{:S(2)}) collective-permute-start(bf16[192,128]{1,0:T(8,128)(2,1)S(1)} %pad_maximum_fusion), channel_id=1, source_target_pairs={{0,16},{1,17},{2,18},{3,19},{4,20},{5,21},{6,22},{7,23},{8,24},{9,... | collective-permute-start | bytes 147464 | tf_op jit(solution)/shard_map/ppermute | solution.py:210
  23.8 14.9 %collective-permute-start = (bf16[192,128]{1,0:T(8,128)(2,1)S(1)}, bf16[192,128]{1,0:T(8,128)(2,1)S(1)}, u32[]{:S(2)}, u32[]{:S(2)}) collective-permute-start(bf16[192,128]{1,0:T(8,128)(2,1)S(1)} %pad_maximum_fusion), channel_id=1, source_target_pairs={{0,0},{1,1},{2,2},{3,3},{4,4},{5,5},{6,6},{7,7},{8,8},{9,9},{10,10... | collective-permute-start | bytes 147464 | tf_op jit(solution)/shard_map/ppermute | solution.py:210
  50.2 26.0 %copy-start = (bf16[1,256,4096]{2,1,0:T(8,128)(2,1)S(1)}, bf16[1,256,4096]{2,1,0:T(8,128)(2,1)}, u32[]{:S(2)}) copy-start(bf16[1,256,4096]{2,1,0:T(8,128)(2,1)} %param.5) | copy-start | bytes 6291460
  50.2 9.7 %collective-permute-start.5 = (bf16[4,392,128]{2,1,0:T(8,128)(2,1)S(1)}, bf16[4,392,128]{2,1,0:T(8,128)(2,1)S(1)}, u32[]{:S(2)}, u32[]{:S(2)}) collective-permute-start(bf16[4,392,128]{2,1,0:T(8,128)(2,1)S(1)} %all_to_all.5.refs_0_), channel_id=1, source_target_pairs={{0,800},{32,192},{96,832},{256,480},{128,928},{544,704},{224,960},... | collective-permute-start | bytes 1204232 | tf_op jit(solution)/shard_map/ppermute | solution.py:230
  53.0 11.1 %collective-permute-start.4 = (bf16[4,392,128]{2,1,0:T(8,128)(2,1)S(1)}, bf16[4,392,128]{2,1,0:T(8,128)(2,1)S(1)}, u32[]{:S(2)}, u32[]{:S(2)}) collective-permute-start(bf16[4,392,128]{2,1,0:T(8,128)(2,1)S(1)} %all_to_all.5.refs_0_), channel_id=1, source_target_pairs={{0,288},{32,64},{96,320},{256,352},{128,416},{544,576},{224,448},{... | collective-permute-start | bytes 1204232 | tf_op jit(solution)/shard_map/ppermute | solution.py:230
  60.6 8.3 %collective-permute-start.7 = (bf16[2,392,128]{2,1,0:T(8,128)(2,1)}, bf16[2,392,128]{2,1,0:T(8,128)(2,1)S(1)}, u32[]{:S(2)}, u32[]{:S(2)}) collective-permute-start(bf16[2,392,128]{2,1,0:T(8,128)(2,1)} %slice.17), channel_id=1, source_target_pairs={{0,800},{32,192},{96,832},{256,480},{128,928},{544,704},{224,960},... | collective-permute-start | bytes 602120 | tf_op jit(solution)/shard_map/ppermute | solution.py:230
  64.8 8.5 %collective-permute-start.6 = (bf16[2,392,128]{2,1,0:T(8,128)(2,1)}, bf16[2,392,128]{2,1,0:T(8,128)(2,1)}, u32[]{:S(2)}, u32[]{:S(2)}) collective-permute-start(bf16[2,392,128]{2,1,0:T(8,128)(2,1)} %slice.16), channel_id=1, source_target_pairs={{0,288},{32,64},{96,320},{256,352},{128,416},{544,576},{224,448},{... | collective-permute-start | bytes 602120 | tf_op jit(solution)/shard_map/ppermute | solution.py:230
  66.8 23.1 %copy-start.1 = (s32[1,128]{1,0:T(1,128)S(1)}, s32[1,128]{1,0:T(1,128)}, u32[]{:S(2)}) copy-start(s32[1,128]{1,0:T(1,128)} %lengths.1) | copy-start | bytes 1540
  66.9 24.5 %collective-permute-start.8 = (bf16[12,392,128]{2,1,0:T(8,128)(2,1)S(1)}, bf16[12,392,128]{2,1,0:T(8,128)(2,1)S(1)}, u32[]{:S(2)}, u32[]{:S(2)}) collective-permute-start(bf16[12,392,128]{2,1,0:T(8,128)(2,1)S(1)} %join.2.joined), channel_id=1, source_target_pairs={{0,32},{32,0},{1,33},{33,1},{2,34},{34,2},{3,35},{35,3},{4,36},{36... | collective-permute-start | bytes 3612680 | tf_op jit(solution)/shard_map/ppermute | solution.py:271
  74.3 17.1 %collective-permute-start.9 = (bf16[4,392,128]{2,1,0:T(8,128)(2,1)S(1)}, bf16[4,392,128]{2,1,0:T(8,128)(2,1)S(1)}, u32[]{:S(2)}, u32[]{:S(2)}) collective-permute-start(bf16[4,392,128]{2,1,0:T(8,128)(2,1)S(1)} %join.3.last), channel_id=1, source_target_pairs={{0,32},{32,0},{1,33},{33,1},{2,34},{34,2},{3,35},{35,3},{4,36},{36... | collective-permute-start | bytes 1204232 | tf_op jit(solution)/shard_map/ppermute | solution.py:272
  76.3 7.8 %collective-permute-start.3 = (bf16[32,4096]{1,0:T(8,128)(2,1)S(1)}, bf16[32,4096]{1,0:T(8,128)(2,1)S(1)}, u32[]{:S(2)}, u32[]{:S(2)}) collective-permute-start(bf16[32,4096]{1,0:T(8,128)(2,1)S(1)} %get-tuple-element.17), channel_id=1, source_target_pairs={{32,0},{64,32},{96,64},{128,96},{160,128},{192,160},{224,192},{256... | collective-permute-start | bytes 786440 | tf_op jit(solution)/shard_map/ppermute | solution.py:250
  80.2 9.8 %collective-permute-start.2 = (bf16[32,4096]{1,0:T(8,128)(2,1)S(1)}, bf16[32,4096]{1,0:T(8,128)(2,1)S(1)}, u32[]{:S(2)}, u32[]{:S(2)}) collective-permute-start(bf16[32,4096]{1,0:T(8,128)(2,1)S(1)} %get-tuple-element.18), channel_id=1, source_target_pairs={{0,32},{32,64},{64,96},{96,128},{128,160},{160,192},{192,224},{224... | collective-permute-start | bytes 786440 | tf_op jit(solution)/shard_map/ppermute | solution.py:249
  90.0 1.4 %copy-start.2 = (s32[1,32]{1,0:T(1,128)S(1)}, s32[1,32]{1,0:T(1,128)}, u32[]{:S(2)}) copy-start(s32[1,32]{1,0:T(1,128)} %shifts.1) | copy-start | bytes 388
where the time goes:
time: 94.7 us; the launch traced here: 94.3 us
  starting transfers between devices  46.2 us (49%)
  waiting for transfers between devices  28.1 us (30%)
  blocking collectives  11.3 us (12%)
  Pallas kernels  5.27 us (6%)
  local copies, waits for them, and re-layouts  2.39 us (3%)
    ppermute x2, starting transfers between devices, moved(): return lax.ppermute(value, (*PLANE, 'z'), pairs)  24.9 us
    ppermute x2, waiting for transfers between devices, moved(): return lax.ppermute(value, (*PLANE, 'z'), pairs)  12.2 us
    ppermute x4, starting transfers between devices, passed_on(): return lax.ppermute(value, PLANE, pairs)  11.6 us
    all_to_all x1, blocking collectives, line_of(): lax.all_to_all(for_each(value, SIDE), PLANE, 0, 0, axis_index_groups=grou...  11.3 us
    ppermute x4, waiting for transfers between devices, passed_on(): return lax.ppermute(value, PLANE, pairs)  8.03 us
    ppermute x1, waiting for transfers between devices, shards(): left = lax.ppermute(tail, PLANE, [(i, i + 1) for i in range(size - 1)])  5.93 us
    ppermute x1, starting transfers between devices, shards(): right = lax.ppermute(head, PLANE, [(i + 1, i) for i in range(size - 1)])  3.9 us
    pallas_call x1, Pallas kernels, attend(): pl.pallas_call(attend_kernel, out_shape=jax.ShapeDtypeStruct((slots.shape...  2.84 us
  transfers between devices with their start and end apart: 10, of which 5 were waited for; matrix products, arithmetic and copies ran while one was open for 2% of the time, Pallas kernels for 3%

commit v1 on v0

--- a/solution.py
+++ b/solution.py
@@ -71,7 +71,7 @@
 
 
 def parts_of(joined, last):
-    return [joined.at[i * SIDE : (i + 1) * SIDE] for i in range(SIDE - 1)] + [last]
+    return [pair.at[i * SIDE : (i + 1) * SIDE] for pair in (joined, last) for i in range(2)]
 
 
 def project_kernel(
@@ -173,9 +173,8 @@
 
 
 def join_kernel(*refs):
-    places = refs[0].shape[0]
     for at, block in enumerate(refs[:-1]):
-        refs[-1][at * places : (at + 1) * places] = block[...]
+        refs[-1][at * SIDE : (at + 1) * SIDE] = block[...]
 
 
 def join(blocks):
@@ -261,12 +260,10 @@
     ).astype(jnp.int32)
     near, far, scalars = lax.optimization_barrier((near, far, scalars))
     tally = jnp.full((8, own.shape[1]), live).astype(jnp.bfloat16)
-    line = line_of(jnp.concatenate([near, far, tally]))
-    after = passed_on(line, 1)
-    ahead = passed_on(line, 3)
-    lower = passed_on(after[: SIDE // 2], 1)
-    higher = passed_on(ahead[SIDE // 2 :], 3)
-    joined, last = join([line, after, ahead]), join([lower, higher])
+    blocks = [line_of(jnp.concatenate([near, far, tally]))]
+    for step in STEPS[1:]:
+        blocks.append(passed_on(blocks[0], step))
+    joined, last = join(blocks[:2]), join(blocks[2:])
     mates = [(0, 1), (1, 0)]
     other_joined = lax.ppermute(joined, "core", mates)
     other_last = lax.ppermute(last, "core", mates)

time: 94.7 us -> 89.7 us (0.947)
  waiting for transfers between devices: 28.1 us -> 24.6 us
  local copies, waits for them, and re-layouts: 2.39 us -> 1 us
    ppermute x4 -> x3, waiting for transfers between devices: 8.03 us -> 4.52 us  [passed_on(): return lax.ppermute(value, PLANE, pairs)]
    ppermute x4 -> x3, starting transfers between devices: 11.6 us -> 9.63 us  [passed_on(): return lax.ppermute(value, PLANE, pairs)]
    ppermute x1, starting transfers between devices: 3.9 us -> 5.57 us  [shards(): right = lax.ppermute(head, PLANE, [(i + 1, i) for i in range(size - 1)])]
    slice x2 -> x0, local copies, waits for them, and re-layouts: 1.39 us -> none  [the longest x1 0.7 us: shards(): lower = passed_on(after[:SIDE // 2], 1)]
  transfers between devices with their start and end apart: 10 -> 9, of which waited for: 5 -> 6; matrix products, arithmetic and copies ran while one was open for 2% -> 0% of each run, Pallas kernels for 3% -> 3%
where the time goes in v1:
time: 89.7 us; the launch traced here: 89.3 us
  starting transfers between devices  45.9 us (51%)
  waiting for transfers between devices  24.6 us (27%)
  blocking collectives  11.5 us (13%)
  Pallas kernels  5.34 us (6%)
  local copies, waits for them, and re-layouts  1 us (1%)
    ppermute x2, starting transfers between devices, moved(): return lax.ppermute(value, (*PLANE, 'z'), pairs)  24.9 us
    ppermute x2, waiting for transfers between devices, moved(): return lax.ppermute(value, (*PLANE, 'z'), pairs)  12.2 us
    all_to_all x1, blocking collectives, line_of(): lax.all_to_all(for_each(value, SIDE), PLANE, 0, 0, axis_index_groups=grou...  11.5 us
    ppermute x3, starting transfers between devices, passed_on(): return lax.ppermute(value, PLANE, pairs)  9.63 us
    ppermute x1, waiting for transfers between devices, shards(): left = lax.ppermute(tail, PLANE, [(i, i + 1) for i in range(size - 1)])  5.93 us
    ppermute x1, starting transfers between devices, shards(): right = lax.ppermute(head, PLANE, [(i + 1, i) for i in range(size - 1)])  5.57 us
    ppermute x3, waiting for transfers between devices, passed_on(): return lax.ppermute(value, PLANE, pairs)  4.52 us
    pallas_call x1, Pallas kernels, attend(): pl.pallas_call(attend_kernel, out_shape=jax.ShapeDtypeStruct((slots.shape...  2.83 us
  transfers between devices with their start and end apart: 9, of which 6 were waited for; matrix products, arithmetic and copies ran while one was open for 0% of the time, Pallas kernels for 3%

profile of v1, /device:TPU:8, one launch (start us, length us, event | category | flops | bytes accessed | tf_op | source)
XLA Modules:
  0.0 89.3 jit_solution(2859915525359618172)
XLA Ops:
  0.0 0.8 constant_dynamic-slice_fusion
  0.8 23.0 %collective-permute-start.1 = (bf16[192,128]{1,0:T(8,128)(2,1)S(1)}, bf16[192,128]{1,0:T(8,128)(2,1)S(1)}, u32[]{:S(2)}, u32[]{:S(2)}) collective-permute-start(bf16[192,128]{1,0:T(8,128)(2,1)S(1)} %pad_maximum_fusion), channel_id=1, source_target_pairs={{0,16},{1,17},{2,18},{3,19},{4,20},{5,21},{6,22},{7,23},{8,24},{9,... | collective-permute-start | bytes 147464 | tf_op jit(solution)/shard_map/ppermute | solution.py:209
  23.8 1.9 %collective-permute-start = (bf16[192,128]{1,0:T(8,128)(2,1)S(1)}, bf16[192,128]{1,0:T(8,128)(2,1)S(1)}, u32[]{:S(2)}, u32[]{:S(2)}) collective-permute-start(bf16[192,128]{1,0:T(8,128)(2,1)S(1)} %pad_maximum_fusion), channel_id=1, source_target_pairs={{0,0},{1,1},{2,2},{3,3},{4,4},{5,5},{6,6},{7,7},{8,8},{9,9},{10,10... | collective-permute-start | bytes 147464 | tf_op jit(solution)/shard_map/ppermute | solution.py:209
  26.4 0.1 stack.23.scalars
  26.5 0.0 collective-permute-done.1
  26.5 12.2 %collective-permute-done = bf16[192,128]{1,0:T(8,128)(2,1)S(1)} collective-permute-done((bf16[192,128]{1,0:T(8,128)(2,1)S(1)}, bf16[192,128]{1,0:T(8,128)(2,1)S(1)}, u32[]{:S(2)}, u32[]{:S(2)}) %collective-permute-start) | collective-permute-done | bytes 49184 | tf_op jit(solution)/shard_map/ppermute | solution.py:209
  38.7 0.1 maximum_maximum_fusion
  38.8 0.1 broadcast_in_dim.13
  38.9 0.0 copy-start
  38.9 11.5 %all_to_all.5.refs_0_ = bf16[4,392,128]{2,1,0:T(8,128)(2,1)S(1)} all-to-all(bf16[4,392,128]{2,1,0:T(8,128)(2,1)S(1)} %broadcast_in_dim.13), channel_id=1, replica_groups={{0,96,128,224},{32,256,544,768},{288,320,416,448},{64,352,576,864},{512..., dimensions={0} | all-to-all | bytes 802816 | tf_op jit(solution)/shard_map/all_to_all | solution.py:218
  50.3 3.4 %collective-permute-start.4 = (bf16[4,392,128]{2,1,0:T(8,128)(2,1)S(1)}, bf16[4,392,128]{2,1,0:T(8,128)(2,1)}, u32[]{:S(2)}, u32[]{:S(2)}) collective-permute-start(bf16[4,392,128]{2,1,0:T(8,128)(2,1)S(1)} %all_to_all.5.refs_0_), channel_id=1, source_target_pairs={{0,288},{32,64},{96,320},{256,352},{128,416},{544,576},{224,448},{... | collective-permute-start | bytes 1204232 | tf_op jit(solution)/shard_map/ppermute | solution.py:229
  53.8 2.6 %collective-permute-start.6 = (bf16[4,392,128]{2,1,0:T(8,128)(2,1)S(1)}, bf16[4,392,128]{2,1,0:T(8,128)(2,1)S(1)}, u32[]{:S(2)}, u32[]{:S(2)}) collective-permute-start(bf16[4,392,128]{2,1,0:T(8,128)(2,1)S(1)} %all_to_all.5.refs_0_), channel_id=1, source_target_pairs={{0,512},{32,160},{96,608},{256,384},{128,640},{544,672},{224,736},... | collective-permute-start | bytes 1204232 | tf_op jit(solution)/shard_map/ppermute | solution.py:229
  56.4 3.6 %collective-permute-start.5 = (bf16[4,392,128]{2,1,0:T(8,128)(2,1)S(1)}, bf16[4,392,128]{2,1,0:T(8,128)(2,1)S(1)}, u32[]{:S(2)}, u32[]{:S(2)}) collective-permute-start(bf16[4,392,128]{2,1,0:T(8,128)(2,1)S(1)} %all_to_all.5.refs_0_), channel_id=1, source_target_pairs={{0,800},{32,192},{96,832},{256,480},{128,928},{544,704},{224,960},... | collective-permute-start | bytes 1204232 | tf_op jit(solution)/shard_map/ppermute | solution.py:229
  60.0 0.0 copy-start.1
  60.0 0.8 collective-permute-done.4.refs_1_
  60.8 1.1 %join.2.joined = bf16[8,392,128]{2,1,0:T(8,128)(2,1)S(1)} custom-call(bf16[4,392,128]{2,1,0:T(8,128)(2,1)S(1)} %all_to_all.5.refs_0_, bf16[4,392,128]{2,1,0:T(8,128)(2,1)} %collective-permute-done.4.refs_1_), custom_call_target="tpu_custom_call" | custom-call | tf_op jit(solution)/shard_map/join/pallas_call | solution.py:182
  61.9 1.9 %collective-permute-start.7 = (bf16[8,392,128]{2,1,0:T(8,128)(2,1)S(1)}, bf16[8,392,128]{2,1,0:T(8,128)(2,1)S(1)}, u32[]{:S(2)}, u32[]{:S(2)}) collective-permute-start(bf16[8,392,128]{2,1,0:T(8,128)(2,1)S(1)} %join.2.joined), channel_id=1, source_target_pairs={{0,32},{32,0},{1,33},{33,1},{2,34},{34,2},{3,35},{35,3},{4,36},{36... | collective-permute-start | bytes 2408456 | tf_op jit(solution)/shard_map/ppermute | solution.py:268
  63.8 1.2 %collective-permute-done.6.refs_1_ = bf16[4,392,128]{2,1,0:T(8,128)(2,1)S(1)} collective-permute-done((bf16[4,392,128]{2,1,0:T(8,128)(2,1)S(1)}, bf16[4,392,128]{2,1,0:T(8,128)(2,1)S(1)}, u32[]{:S(2)}, u32[]{:S(2)}) %collective-permute-start.6) | collective-permute-done | bytes 401440 | tf_op jit(solution)/shard_map/ppermute | solution.py:229
  65.0 2.5 %collective-permute-done.5.refs_0_ = bf16[4,392,128]{2,1,0:T(8,128)(2,1)S(1)} collective-permute-done((bf16[4,392,128]{2,1,0:T(8,128)(2,1)S(1)}, bf16[4,392,128]{2,1,0:T(8,128)(2,1)S(1)}, u32[]{:S(2)}, u32[]{:S(2)}) %collective-permute-start.5) | collective-permute-done | bytes 401440 | tf_op jit(solution)/shard_map/ppermute | solution.py:229
  67.5 0.1 join.3.last
  67.6 1.9 %collective-permute-start.8 = (bf16[8,392,128]{2,1,0:T(8,128)(2,1)S(1)}, bf16[8,392,128]{2,1,0:T(8,128)(2,1)S(1)}, u32[]{:S(2)}, u32[]{:S(2)}) collective-permute-start(bf16[8,392,128]{2,1,0:T(8,128)(2,1)S(1)} %join.3.last), channel_id=1, source_target_pairs={{0,32},{32,0},{1,33},{33,1},{2,34},{34,2},{3,35},{35,3},{4,36},{36... | collective-permute-start | bytes 2408456 | tf_op jit(solution)/shard_map/ppermute | solution.py:269
  69.5 0.0 copy-done
  69.5 0.1 dynamic-slice_bitcast_fusion
  69.6 5.6 %collective-permute-start.3 = (bf16[32,4096]{1,0:T(8,128)(2,1)S(1)}, bf16[32,4096]{1,0:T(8,128)(2,1)S(1)}, u32[]{:S(2)}, u32[]{:S(2)}) collective-permute-start(bf16[32,4096]{1,0:T(8,128)(2,1)S(1)} %get-tuple-element.17), channel_id=1, source_target_pairs={{32,0},{64,32},{96,64},{128,96},{160,128},{192,160},{224,192},{256... | collective-permute-start | bytes 786440 | tf_op jit(solution)/shard_map/ppermute | solution.py:249
  75.2 1.9 %collective-permute-start.2 = (bf16[32,4096]{1,0:T(8,128)(2,1)S(1)}, bf16[32,4096]{1,0:T(8,128)(2,1)S(1)}, u32[]{:S(2)}, u32[]{:S(2)}) collective-permute-start(bf16[32,4096]{1,0:T(8,128)(2,1)S(1)} %get-tuple-element.18), channel_id=1, source_target_pairs={{0,32},{32,64},{64,96},{96,128},{128,160},{160,192},{192,224},{224... | collective-permute-start | bytes 786440 | tf_op jit(solution)/shard_map/ppermute | solution.py:248
  77.1 1.9 %collective-permute-done.3.right = bf16[32,4096]{1,0:T(8,128)(2,1)S(1)} collective-permute-done((bf16[32,4096]{1,0:T(8,128)(2,1)S(1)}, bf16[32,4096]{1,0:T(8,128)(2,1)S(1)}, u32[]{:S(2)}, u32[]{:S(2)}) %collective-permute-start.3) | collective-permute-done | bytes 262176 | tf_op jit(solution)/shard_map/ppermute | solution.py:249
  79.0 5.9 %collective-permute-done.2.left = bf16[32,4096]{1,0:T(8,128)(2,1)S(1)} collective-permute-done((bf16[32,4096]{1,0:T(8,128)(2,1)S(1)}, bf16[32,4096]{1,0:T(8,128)(2,1)S(1)}, u32[]{:S(2)}, u32[]{:S(2)}) %collective-permute-start.2) | collective-permute-done | bytes 262176 | tf_op jit(solution)/shard_map/ppermute | solution.py:248
  85.0 0.0 copy-done.1
  85.0 1.4 %project.1 = (f32[320,384]{1,0:T(8,128)S(1)}, f32[8,128]{1,0:T(8,128)S(1)}, s32[8,128]{1,0:T(8,128)S(1)}) custom-call(s32[5]{0:T(128)S(1)} %stack.23.scalars, bf16[256,4096]{1,0:T(8,128)(2,1)S(1)} %bitcast.16, bf16[32,4096]{1,0:T(8,128)(2,1)S(1)} %collective-permute-done.2.left, bf16[32,4096]{1,0:T(8,128)(2,1)S(1)} %collective-permute-done.3.right, ...), custom_call_target="tpu_custom_call" | custom-call | flops 503316480 | tf_op jit(solution)/shard_map/project/pallas_call | solution.py:96
  86.4 0.0 collective-permute-done.7.joined
  86.4 0.0 collective-permute-done.8.last
  86.4 2.8 %attend.1 = bf16[256,128]{1,0:T(8,128)(2,1)} custom-call(s32[5]{0:T(128)S(1)} %stack.23.scalars, s32[1,1]{1,0:T(1,128)} %copy.6.pads, s32[1,32]{1,0:T(1,128)S(1)} %copy-done.2, bf16[256,4096]{1,0:T(8,128)(2,1)S(1)} %bitcast.17, bf16[32,4096]{1,0:T(8,128)(2,1)S(1)} %collective-permute-done.2.left, bf16[32,4096]{1,0:T(8,128)(2,1)S(1)} %collective-permute-done.3.right, ...), custom_call_target="tpu_custom_call" | custom-call | tf_op jit(solution)/shard_map/attend/pallas_call | solution.py:164
  (5 shorter events, 0.0 us)
Async XLA Ops:
  0.8 25.7 %collective-permute-start.1 = (bf16[192,128]{1,0:T(8,128)(2,1)S(1)}, bf16[192,128]{1,0:T(8,128)(2,1)S(1)}, u32[]{:S(2)}, u32[]{:S(2)}) collective-permute-start(bf16[192,128]{1,0:T(8,128)(2,1)S(1)} %pad_maximum_fusion), channel_id=1, source_target_pairs={{0,16},{1,17},{2,18},{3,19},{4,20},{5,21},{6,22},{7,23},{8,24},{9,... | collective-permute-start | bytes 147464 | tf_op jit(solution)/shard_map/ppermute | solution.py:209
  23.8 14.9 %collective-permute-start = (bf16[192,128]{1,0:T(8,128)(2,1)S(1)}, bf16[192,128]{1,0:T(8,128)(2,1)S(1)}, u32[]{:S(2)}, u32[]{:S(2)}) collective-permute-start(bf16[192,128]{1,0:T(8,128)(2,1)S(1)} %pad_maximum_fusion), channel_id=1, source_target_pairs={{0,0},{1,1},{2,2},{3,3},{4,4},{5,5},{6,6},{7,7},{8,8},{9,9},{10,10... | collective-permute-start | bytes 147464 | tf_op jit(solution)/shard_map/ppermute | solution.py:209
  38.9 30.6 %copy-start = (bf16[1,256,4096]{2,1,0:T(8,128)(2,1)S(1)}, bf16[1,256,4096]{2,1,0:T(8,128)(2,1)}, u32[]{:S(2)}) copy-start(bf16[1,256,4096]{2,1,0:T(8,128)(2,1)} %param.5) | copy-start | bytes 6291460
  50.3 10.5 %collective-permute-start.4 = (bf16[4,392,128]{2,1,0:T(8,128)(2,1)S(1)}, bf16[4,392,128]{2,1,0:T(8,128)(2,1)}, u32[]{:S(2)}, u32[]{:S(2)}) collective-permute-start(bf16[4,392,128]{2,1,0:T(8,128)(2,1)S(1)} %all_to_all.5.refs_0_), channel_id=1, source_target_pairs={{0,288},{32,64},{96,320},{256,352},{128,416},{544,576},{224,448},{... | collective-permute-start | bytes 1204232 | tf_op jit(solution)/shard_map/ppermute | solution.py:229
  53.8 11.3 %collective-permute-start.6 = (bf16[4,392,128]{2,1,0:T(8,128)(2,1)S(1)}, bf16[4,392,128]{2,1,0:T(8,128)(2,1)S(1)}, u32[]{:S(2)}, u32[]{:S(2)}) collective-permute-start(bf16[4,392,128]{2,1,0:T(8,128)(2,1)S(1)} %all_to_all.5.refs_0_), channel_id=1, source_target_pairs={{0,512},{32,160},{96,608},{256,384},{128,640},{544,672},{224,736},... | collective-permute-start | bytes 1204232 | tf_op jit(solution)/shard_map/ppermute | solution.py:229
  56.4 11.2 %collective-permute-start.5 = (bf16[4,392,128]{2,1,0:T(8,128)(2,1)S(1)}, bf16[4,392,128]{2,1,0:T(8,128)(2,1)S(1)}, u32[]{:S(2)}, u32[]{:S(2)}) collective-permute-start(bf16[4,392,128]{2,1,0:T(8,128)(2,1)S(1)} %all_to_all.5.refs_0_), channel_id=1, source_target_pairs={{0,800},{32,192},{96,832},{256,480},{128,928},{544,704},{224,960},... | collective-permute-start | bytes 1204232 | tf_op jit(solution)/shard_map/ppermute | solution.py:229
  60.0 25.0 %copy-start.1 = (s32[1,128]{1,0:T(1,128)S(1)}, s32[1,128]{1,0:T(1,128)}, u32[]{:S(2)}) copy-start(s32[1,128]{1,0:T(1,128)} %lengths.1) | copy-start | bytes 1540
  61.9 24.5 %collective-permute-start.7 = (bf16[8,392,128]{2,1,0:T(8,128)(2,1)S(1)}, bf16[8,392,128]{2,1,0:T(8,128)(2,1)S(1)}, u32[]{:S(2)}, u32[]{:S(2)}) collective-permute-start(bf16[8,392,128]{2,1,0:T(8,128)(2,1)S(1)} %join.2.joined), channel_id=1, source_target_pairs={{0,32},{32,0},{1,33},{33,1},{2,34},{34,2},{3,35},{35,3},{4,36},{36... | collective-permute-start | bytes 2408456 | tf_op jit(solution)/shard_map/ppermute | solution.py:268
  67.6 18.8 %collective-permute-start.8 = (bf16[8,392,128]{2,1,0:T(8,128)(2,1)S(1)}, bf16[8,392,128]{2,1,0:T(8,128)(2,1)S(1)}, u32[]{:S(2)}, u32[]{:S(2)}) collective-permute-start(bf16[8,392,128]{2,1,0:T(8,128)(2,1)S(1)} %join.3.last), channel_id=1, source_target_pairs={{0,32},{32,0},{1,33},{33,1},{2,34},{34,2},{3,35},{35,3},{4,36},{36... | collective-permute-start | bytes 2408456 | tf_op jit(solution)/shard_map/ppermute | solution.py:269
  69.6 9.4 %collective-permute-start.3 = (bf16[32,4096]{1,0:T(8,128)(2,1)S(1)}, bf16[32,4096]{1,0:T(8,128)(2,1)S(1)}, u32[]{:S(2)}, u32[]{:S(2)}) collective-permute-start(bf16[32,4096]{1,0:T(8,128)(2,1)S(1)} %get-tuple-element.17), channel_id=1, source_target_pairs={{32,0},{64,32},{96,64},{128,96},{160,128},{192,160},{224,192},{256... | collective-permute-start | bytes 786440 | tf_op jit(solution)/shard_map/ppermute | solution.py:249
  75.2 9.8 %collective-permute-start.2 = (bf16[32,4096]{1,0:T(8,128)(2,1)S(1)}, bf16[32,4096]{1,0:T(8,128)(2,1)S(1)}, u32[]{:S(2)}, u32[]{:S(2)}) collective-permute-start(bf16[32,4096]{1,0:T(8,128)(2,1)S(1)} %get-tuple-element.18), channel_id=1, source_target_pairs={{0,32},{32,64},{64,96},{96,128},{128,160},{160,192},{192,224},{224... | collective-permute-start | bytes 786440 | tf_op jit(solution)/shard_map/ppermute | solution.py:248
  85.0 1.4 %copy-start.2 = (s32[1,32]{1,0:T(1,128)S(1)}, s32[1,32]{1,0:T(1,128)}, u32[]{:S(2)}) copy-start(s32[1,32]{1,0:T(1,128)} %shifts.1) | copy-start | bytes 388
